TPU v7x, 32 devices: a whole 2x2x4 slice. The times are simulated.
32 devices in a mesh: shard: 16 (over z, y, x), mp: 2 (over core).
Axes of the slice: x: 2, y: 2, z: 4, core: 2. Of those that a mesh axis runs over, the one named last changes fastest.
Arguments:
- item_rows: float32 [4096, 256], P('shard', 'mp'), may hold values from -6 to 6
- first_moment: float32 [4096, 256], P('shard', 'mp'), may hold values from -2 to 2
- second_moment: float32 [4096, 256], P('shard', 'mp'), may hold values from 0.01 to 4
- item_cot: bfloat16 [4096, 256], P('shard', 'mp'), may hold values from -6 to 6
- tile_bits: int32 [256, 8, 128], P('shard'), may hold values from 0 to 65535, as said below
- tile_item: int32 [256], P('shard'), may hold values from 0 to 1
- tile_dest: int32 [256], P('shard'), may hold values from 0 to 15
- basket_gain: float32 [256], replicated, may hold values from 0.1 to 1.9
- item_gain: float32 [256], replicated, may hold values from 0.1 to 1.9
- gate_basket: bfloat16 [256, 2048], P(None, 'mp'), may hold values from -0.375 to 0.375
- up_basket: bfloat16 [256, 2048], P(None, 'mp'), may hold values from -0.375 to 0.375
- down_basket: bfloat16 [2048, 256], P('mp'), may hold values from -0.125 to 0.125
- gate_item: bfloat16 [256, 2048], P(None, 'mp'), may hold values from -0.375 to 0.375
- up_item: bfloat16 [256, 2048], P(None, 'mp'), may hold values from -0.375 to 0.375
- down_item: bfloat16 [2048, 256], P('mp'), may hold values from -0.125 to 0.125
Outputs:
- new_rows: float32 [4096, 256], P('shard', 'mp')
- new_first: float32 [4096, 256], P('shard', 'mp')
- new_second: float32 [4096, 256], P('shard', 'mp')
Inputs may be any that keep to these rules, and one draw needn't show every extreme that they name: `tile_bits`: each word holds 16 independent incidence bits in its low bits.
All inputs are finite; a program needn't handle non-finite values.
Results may differ from a plain program's by a relative error of at most 0.007.
Values may be sent and summed in bfloat16 or wider, within the bound.
No kernel may reach another device: no remote copies, remote signals or barrier semaphores. Data moves between devices by JAX's collectives and lax.ppermute only.
A program may use at most 128 MiB of HBM per device.

v0:
```python
import jax
import jax.numpy as jnp
from jax import lax
from jax.sharding import PartitionSpec as P

D = 256
BLOCK = 128
NORM_EPSILON = 1e-05
LEARNING_RATE = 0.01
BETA_FIRST = 0.9
BETA_SECOND = 0.99
ADAM_EPSILON = 1e-08


def unpack_tiles(packed):
    shifts = jnp.arange(16, dtype=jnp.int32)
    bit_values = jnp.right_shift(packed[:, :, None, :], shifts[None, None, :, None]) & 1
    return bit_values.reshape(packed.shape[0], packed.shape[1] * 16, packed.shape[2]).astype(
        jnp.bfloat16
    )


def silu_parts(gate_values):
    sigmoid = jax.nn.sigmoid(gate_values)
    return (gate_values * sigmoid, sigmoid * (1.0 + gate_values * (1.0 - sigmoid)))


def rms_scale(values):
    return lax.rsqrt(jnp.mean(values * values, axis=-1, keepdims=True) + NORM_EPSILON)


def owner_sums(partials, tile_dest):
    block_total = lax.axis_size("shard")
    coalesced = jax.ops.segment_sum(partials, tile_dest, num_segments=block_total)
    received = lax.all_to_all(
        coalesced.astype(jnp.bfloat16), "shard", split_axis=0, concat_axis=0, tiled=True
    ).astype(coalesced.dtype)
    return jnp.sum(received, axis=0)


def spread_items(owned, masks, tile_item, tile_dest, item_blocks):
    gathered = lax.all_gather(owned, "shard", axis=0, tiled=True)
    gathered = gathered.reshape(-1, BLOCK, owned.shape[1])
    selected = jnp.take(gathered, tile_dest, axis=0)
    contrib = jnp.einsum("tib,tbf->tif", masks, selected, preferred_element_type=jnp.float32)
    summed = jax.ops.segment_sum(contrib, tile_item, num_segments=item_blocks)
    return summed.reshape(item_blocks * BLOCK, owned.shape[1])


def whole_features(values):
    return lax.all_gather(values.astype(jnp.bfloat16), "mp", axis=1, tiled=True).astype(
        values.dtype
    )


def local(
    item_rows,
    first_moment,
    second_moment,
    item_cot,
    tile_bits,
    tile_item,
    tile_dest,
    basket_gain,
    item_gain,
    gate_basket,
    up_basket,
    down_basket,
    gate_item,
    up_item,
    down_item,
):
    half_width = item_rows.shape[1]
    item_blocks = item_rows.shape[0] // BLOCK
    offset = lax.axis_index("mp") * half_width
    masks = unpack_tiles(tile_bits)
    rows_blocks = item_rows.astype(jnp.bfloat16).reshape(item_blocks, BLOCK, half_width)
    picked = jnp.take(rows_blocks, tile_item, axis=0)
    partials = jnp.einsum("tib,tif->tbf", masks, picked, preferred_element_type=jnp.float32)
    basket_sum = owner_sums(partials, tile_dest)
    sum_full = whole_features(basket_sum)
    scale_basket = rms_scale(sum_full)
    normed = sum_full * scale_basket * basket_gain
    normed_bf = normed.astype(jnp.bfloat16)
    gate_pre = jnp.dot(normed_bf, gate_basket, preferred_element_type=jnp.float32)
    up_pre = jnp.dot(normed_bf, up_basket, preferred_element_type=jnp.float32)
    silu_value, silu_slope = silu_parts(gate_pre)
    hidden = (silu_value * up_pre).astype(jnp.bfloat16)
    down_part = jnp.dot(hidden, down_basket, preferred_element_type=jnp.float32)
    down_mine = lax.psum_scatter(
        down_part.astype(jnp.bfloat16), "mp", scatter_dimension=1, tiled=True
    ).astype(jnp.float32)
    basket_out = (lax.dynamic_slice_in_dim(normed, offset, half_width, 1) + down_mine).astype(
        jnp.bfloat16
    )
    message = spread_items(basket_out, masks, tile_item, tile_dest, item_blocks)
    message_full = lax.all_gather(message, "mp", axis=1, tiled=True)
    scale_item = rms_scale(message_full)
    query = (message_full * scale_item * item_gain).astype(jnp.bfloat16)
    gate_item_pre = jnp.dot(query, gate_item, preferred_element_type=jnp.float32)
    up_item_pre = jnp.dot(query, up_item, preferred_element_type=jnp.float32)
    item_value, item_slope = silu_parts(gate_item_pre)
    cot_full = lax.all_gather(item_cot, "mp", axis=1, tiled=True)
    grad_hidden = jnp.einsum("rd,hd->rh", cot_full, down_item, preferred_element_type=jnp.float32)
    grad_up = (grad_hidden * item_value).astype(jnp.bfloat16)
    grad_gate = (grad_hidden * up_item_pre * item_slope).astype(jnp.bfloat16)
    query_part = jnp.einsum(
        "rh,dh->rd", grad_gate, gate_item, preferred_element_type=jnp.float32
    ) + jnp.einsum("rh,dh->rd", grad_up, up_item, preferred_element_type=jnp.float32)
    gain_mine = lax.dynamic_slice_in_dim(item_gain, offset, half_width, 0)
    grad_query = lax.psum_scatter(
        query_part.astype(jnp.bfloat16), "mp", scatter_dimension=1, tiled=True
    ).astype(jnp.float32)
    inner = lax.psum(jnp.sum(gain_mine * grad_query * message, axis=1, keepdims=True), "mp")
    cubed_item = scale_item * scale_item * scale_item
    grad_message = (scale_item * gain_mine * grad_query - message * cubed_item * inner / D).astype(
        jnp.bfloat16
    )
    grad_blocks = grad_message.reshape(item_blocks, BLOCK, half_width)
    grad_picked = jnp.take(grad_blocks, tile_item, axis=0)
    grad_partials = jnp.einsum(
        "tib,tif->tbf", masks, grad_picked, preferred_element_type=jnp.float32
    )
    grad_out = owner_sums(grad_partials, tile_dest)
    grad_out_full = whole_features(grad_out)
    grad_out_bf = grad_out_full.astype(jnp.bfloat16)
    grad_basket_hidden = jnp.einsum(
        "bd,hd->bh", grad_out_bf, down_basket, preferred_element_type=jnp.float32
    )
    grad_basket_up = (grad_basket_hidden * silu_value).astype(jnp.bfloat16)
    grad_basket_gate = (grad_basket_hidden * up_pre * silu_slope).astype(jnp.bfloat16)
    normed_part = jnp.einsum(
        "bh,dh->bd", grad_basket_gate, gate_basket, preferred_element_type=jnp.float32
    ) + jnp.einsum("bh,dh->bd", grad_basket_up, up_basket, preferred_element_type=jnp.float32)
    grad_normed = grad_out_full + lax.psum(normed_part.astype(jnp.bfloat16), "mp").astype(
        jnp.float32
    )
    inner_basket = jnp.sum(basket_gain * grad_normed * sum_full, axis=1, keepdims=True)
    cubed_basket = scale_basket * scale_basket * scale_basket
    grad_sum = scale_basket * basket_gain * grad_normed - sum_full * cubed_basket * inner_basket / D
    grad_sum_mine = lax.dynamic_slice_in_dim(grad_sum, offset, half_width, 1).astype(jnp.bfloat16)
    back_items = spread_items(grad_sum_mine, masks, tile_item, tile_dest, item_blocks)
    gradient = item_cot.astype(jnp.float32) + back_items
    new_first = BETA_FIRST * first_moment + (1.0 - BETA_FIRST) * gradient
    new_second = BETA_SECOND * second_moment + (1.0 - BETA_SECOND) * gradient * gradient
    new_rows = item_rows - LEARNING_RATE * new_first / (jnp.sqrt(new_second) + ADAM_EPSILON)
    return (new_rows, new_first, new_second)


def solution(mesh):
    return jax.shard_map(
        local,
        mesh=mesh,
        in_specs=(
            P("shard", "mp"),
            P("shard", "mp"),
            P("shard", "mp"),
            P("shard", "mp"),
            P("shard", None, None),
            P("shard"),
            P("shard"),
            P(),
            P(),
            P(None, "mp"),
            P(None, "mp"),
            P("mp", None),
            P(None, "mp"),
            P(None, "mp"),
            P("mp", None),
        ),
        out_specs=(P("shard", "mp"), P("shard", "mp"), P("shard", "mp")),
        check_vma=False,
    )
```

profile of v0, /device:TPU:0, one launch (start us, length us, event | category | flops | bytes accessed | tf_op | source)
XLA Modules:
  0.0 214.6 jit_solution(4999208334677294689)
XLA Ops:
  8.0 0.9 convert_element_type.76
  10.9 1.6 scatter_fusion
  13.4 8.5 %all-to-all-start = ((bf16[16,128,128]{2,1,0:T(8,128)(2,1)}), bf16[16,128,128]{2,1,0:T(8,128)(2,1)S(1)}, u32[]{:S(2)}, u32[]{:S(2)}) async-start(bf16[16,128,128]{2,1,0:T(8,128)(2,1)} %convert_element_type.77), calls=%async_computation | async-start | bytes 1048576 | tf_op jit(solution)/shard_map/all_to_all | solution.py:35
  22.0 1.9 all_gather.21
  24.0 1.3 fusion.56
  25.3 11.7 %all-to-all-done = bf16[16,128,128]{2,1,0:T(8,128)(2,1)S(1)} async-done(((bf16[16,128,128]{2,1,0:T(8,128)(2,1)}), bf16[16,128,128]{2,1,0:T(8,128)(2,1)S(1)}, u32[]{:S(2)}, u32[]{:S(2)}) %all-to-all-start) | async-done | bytes 524320 | tf_op jit(solution)/shard_map/all_to_all | solution.py:35
  37.1 1.9 all_gather.18
  43.6 5.9 %reduce-scatter.7.cloned.1.call-done = bf16[128,128]{1,0:T(8,128)(2,1)} async-done(((bf16[256,128]{1,0:T(8,128)(2,1)}), bf16[128,128]{1,0:T(8,128)(2,1)}) %reduce-scatter.7.cloned.1.call-update) | async-done | bytes 32784
  50.4 44.0 %all_gather.19 = bf16[2048,128]{1,0:T(8,128)(2,1)S(1)} all-gather(bf16[128,128]{1,0:T(8,128)(2,1)S(1)} %add_convert_fusion), channel_id=1, replica_groups=mesh['shard'=16,'mp'=2] {'shard'}, dimensions={0}, use_global_device_ids=true | all-gather | bytes 557056 | tf_op jit(solution)/shard_map/all_gather | solution.py:42
  95.4 1.6 scatter_fusion.1
  97.0 2.0 all_gather.20
  100.9 2.0 fusion.2
  102.9 1.7 fusion.3
  105.5 3.5 %reduce-scatter.9.cloned.1.call-done = bf16[128,256]{1,0:T(8,128)(2,1)} async-done(((bf16[256,256]{1,0:T(8,128)(2,1)}), bf16[128,256]{1,0:T(8,128)(2,1)}) %reduce-scatter.9.cloned.1.call-update) | async-done | bytes 65552
  109.0 0.9 copy.29
  110.1 2.5 %psum.14 = f32[256]{0:T(256)S(1)} all-reduce(f32[256]{0:T(256)S(1)} %fusion.33), channel_id=1, replica_groups=mesh['shard'=16,'mp'=2] {'mp'}, use_global_device_ids=true, to_apply=%region_8.11 | all-reduce | flops 256 | bytes 2048 | tf_op jit(solution)/shard_map/psum | solution.py:114
  113.9 1.6 scatter_fusion.2
  115.6 22.2 %all_to_all.10 = bf16[16,128,128]{2,1,0:T(8,128)(2,1)S(1)} all-to-all(bf16[16,128,128]{2,1,0:T(8,128)(2,1)S(1)} %convert_element_type.90), channel_id=1, replica_groups=mesh['shard'=16,'mp'=2] {'shard'}, dimensions={0} | all-to-all | bytes 1048576 | tf_op jit(solution)/shard_map/all_to_all | solution.py:35
  137.8 2.0 all_gather.22
  142.1 1.0 fusion.4
  143.2 16.2 %all-reduce.2.cloned.1.call-done = bf16[128,256]{1,0:T(8,128)(2,1)} async-done(((bf16[128,256]{1,0:T(8,128)(2,1)}), bf16[128,256]{1,0:T(8,128)(2,1)}) %all-reduce.2.cloned.1.call-update) | async-done | bytes 65552 | tf_op jit(solution)/shard_map/psum | solution.py:135
  159.4 1.0 multiply_reduce_fusion.1
  160.5 44.1 %all_gather.23 = bf16[2048,128]{1,0:T(8,128)(2,1)S(1)} all-gather(bf16[128,128]{1,0:T(8,128)(2,1)S(1)} %fusion.38), channel_id=1, replica_groups=mesh['shard'=16,'mp'=2] {'shard'}, dimensions={0}, use_global_device_ids=true | all-gather | bytes 557056 | tf_op jit(solution)/shard_map/all_gather | solution.py:42
  205.7 1.6 scatter_fusion.3
  (97 shorter events, 18.9 us)
Async XLA Ops:
  7.2 92.0 %copy-start = (bf16[256,1024]{1,0:T(8,128)(2,1)S(1)}, bf16[256,1024]{1,0:T(8,128)(2,1)}, u32[]{:S(2)}) copy-start(bf16[256,1024]{1,0:T(8,128)(2,1)} %param.31) | copy-start | bytes 1572868
  7.2 0.7 copy-start.19
  8.0 1.0 copy-start.16
  13.4 8.5 %copy-start.13 = (bf16[256,128]{1,0:T(8,128)(2,1)S(1)}, bf16[256,128]{1,0:T(8,128)(2,1)}, u32[]{:S(2)}) copy-start(bf16[256,128]{1,0:T(8,128)(2,1)} %param.22) | copy-start | bytes 196612
  13.4 10.5 %copy-start.10 = (bf16[1024,256]{1,0:T(8,128)(2,1)S(1)}, bf16[1024,256]{1,0:T(8,128)(2,1)}, u32[]{:S(2)}) copy-start(bf16[1024,256]{1,0:T(8,128)(2,1)} %param.33) | copy-start | bytes 1572868
  13.4 23.6 %all-to-all-start = ((bf16[16,128,128]{2,1,0:T(8,128)(2,1)}), bf16[16,128,128]{2,1,0:T(8,128)(2,1)S(1)}, u32[]{:S(2)}, u32[]{:S(2)}) async-start(bf16[16,128,128]{2,1,0:T(8,128)(2,1)} %convert_element_type.77), calls=%async_computation | async-start | bytes 1048576 | tf_op jit(solution)/shard_map/all_to_all | solution.py:35
  21.9 27.6 %reduce-scatter.7.cloned.1.call-start = ((), (), s32[]{:S(2)}) async-start(), calls=%async_computation.5 | async-start | bytes 98304
  25.3 13.8 %copy-start.1 = (bf16[256,1024]{1,0:T(8,128)(2,1)S(1)}, bf16[256,1024]{1,0:T(8,128)(2,1)}, u32[]{:S(2)}) copy-start(bf16[256,1024]{1,0:T(8,128)(2,1)} %param.28) | copy-start | bytes 1572868
  39.1 0.7 copy-start.17
  39.8 1.0 copy-start.3
  40.8 0.8 copy-start.5
  40.8 1.6 copy-start.11
  41.6 0.8 copy-start.7
  43.5 65.5 %reduce-scatter.9.cloned.1.call-start = ((), (), s32[]{:S(2)}) async-start(), calls=%async_computation.6 | async-start | bytes 196608
  99.8 1.0 copy-start.21
  105.3 54.1 %all-reduce.2.cloned.1.call-start = ((), (), s32[]{:S(2)}) async-start(), calls=%async_computation.4 | async-start | bytes 131072 | tf_op jit(solution)/shard_map/psum | solution.py:135
  115.6 24.3 %copy-start.12 = (bf16[1024,256]{1,0:T(8,128)(2,1)S(1)}, bf16[1024,256]{1,0:T(8,128)(2,1)}, u32[]{:S(2)}) copy-start(bf16[1024,256]{1,0:T(8,128)(2,1)} %param.30) | copy-start | bytes 1572868
  137.8 2.4 %copy-start.8 = (f32[128,1024]{1,0:T(8,128)S(1)}, f32[128,1024]{1,0:T(8,128)}, u32[]{:S(2)}) copy-start(f32[128,1024]{1,0:T(8,128)} %copy-done.7) | copy-start | bytes 1572868
  139.9 1.0 copy-start.2
  139.9 1.2 copy-start.6
  141.1 1.0 copy-start.4
  205.6 1.6 copy-start.9
  205.6 1.6 copy-start.14
  205.6 1.6 copy-start.15
  (2 other events, 1.3 us)
Sparse Core Ops, SparseCore 0:
  43.6 5.8 reduce-scatter.6
  105.5 3.4 reduce-scatter.8
  143.2 16.1 all-reduce.1
where the time goes:
time: 215 us
  blocking collectives  121 us (56%)
  waiting for transfers between devices  37.4 us (17%)
  between operations  14.2 us (7%)
  local copies, waits for them, and re-layouts  12.6 us (6%)
  other arithmetic  12 us (6%)
  matrix products  9.28 us (4%)
  starting transfers between devices  8.6 us (4%)
    all_gather x2, blocking collectives, spread_items(): gathered = lax.all_gather(owned, 'shard', axis=0, tiled=True)  88 us
    all_to_all x1, blocking collectives, owner_sums(): lax.all_to_all(coalesced.astype(jnp.bfloat16), 'shard', split_axis=0, con...  22.2 us
    psum x1, waiting for transfers between devices, local(): lax.psum(normed_part.astype(jnp.bfloat16), 'mp').astype(jnp.float32)  16.2 us
    all_to_all x1, waiting for transfers between devices, owner_sums(): lax.all_to_all(coalesced.astype(jnp.bfloat16), 'shard', split_axis=0, con...  11.7 us
    unnamed x48, local copies, waits for them, and re-layouts  9.61 us
    unnamed x5, waiting for transfers between devices  9.45 us
    all_to_all x1, starting transfers between devices, owner_sums(): lax.all_to_all(coalesced.astype(jnp.bfloat16), 'shard', split_axis=0, con...  8.47 us
  transfers between devices with their start and end apart: 4, of which 4 were waited for; matrix products, arithmetic and copies ran while one was open for 1% of the time, Pallas kernels for 0%

commit v1 on v0

--- a/solution.py
+++ b/solution.py
@@ -132,9 +132,9 @@
     normed_part = jnp.einsum(
         "bh,dh->bd", grad_basket_gate, gate_basket, preferred_element_type=jnp.float32
     ) + jnp.einsum("bh,dh->bd", grad_basket_up, up_basket, preferred_element_type=jnp.float32)
-    grad_normed = grad_out_full + lax.psum(normed_part.astype(jnp.bfloat16), "mp").astype(
-        jnp.float32
-    )
+    grad_normed = grad_out_full + jnp.sum(
+        lax.all_gather(normed_part.astype(jnp.bfloat16), "mp"), axis=0
+    ).astype(jnp.float32)
     inner_basket = jnp.sum(basket_gain * grad_normed * sum_full, axis=1, keepdims=True)
     cubed_basket = scale_basket * scale_basket * scale_basket
     grad_sum = scale_basket * basket_gain * grad_normed - sum_full * cubed_basket * inner_basket / D

time: 215 us -> 198 us (0.921)
  blocking collectives: 121 us -> 97.4 us
  starting transfers between devices: 8.6 us -> 15.4 us
    all_to_all x1 -> x0, blocking collectives: 22.2 us -> none  [owner_sums(): lax.all_to_all(coalesced.astype(jnp.bfloat16), 'shard', split_axis=0, con...]
    psum x1 -> x0, waiting for transfers between devices: 16.2 us -> none  [local(): lax.psum(normed_part.astype(jnp.bfloat16), 'mp').astype(jnp.float32)]
    all_to_all x1 -> x2, waiting for transfers between devices: 11.7 us -> 27.1 us  [owner_sums(): lax.all_to_all(coalesced.astype(jnp.bfloat16), 'shard', split_axis=0, con...]
    all_to_all x1 -> x2, starting transfers between devices: 8.47 us -> 15.4 us  [owner_sums(): lax.all_to_all(coalesced.astype(jnp.bfloat16), 'shard', split_axis=0, con...]
    all_gather x2, blocking collectives: 88 us -> 85.2 us  [spread_items(): gathered = lax.all_gather(owned, 'shard', axis=0, tiled=True)]
    unnamed x5 -> x4, waiting for transfers between devices: 9.45 us -> 9.49 us
where the time goes in v1:
time: 198 us; the launch traced here: 197 us
  blocking collectives  97.4 us (49%)
  waiting for transfers between devices  36.6 us (18%)
  starting transfers between devices  15.4 us (8%)
  between operations  14.5 us (7%)
  local copies, waits for them, and re-layouts  12.6 us (6%)
  other arithmetic  12 us (6%)
  matrix products  8.64 us (4%)
    all_gather x2, blocking collectives, spread_items(): gathered = lax.all_gather(owned, 'shard', axis=0, tiled=True)  85.2 us
    all_to_all x2, waiting for transfers between devices, owner_sums(): lax.all_to_all(coalesced.astype(jnp.bfloat16), 'shard', split_axis=0, con...  27.1 us
    all_to_all x2, starting transfers between devices, owner_sums(): lax.all_to_all(coalesced.astype(jnp.bfloat16), 'shard', split_axis=0, con...  15.4 us
    unnamed x48, local copies, waits for them, and re-layouts  9.6 us
    unnamed x4, waiting for transfers between devices  9.49 us
  transfers between devices with their start and end apart: 4, of which 4 were waited for; matrix products, arithmetic and copies ran while one was open for 1% of the time, Pallas kernels for 0%

profile of v1, /device:TPU:0, one launch (start us, length us, event | category | flops | bytes accessed | tf_op | source)
XLA Modules:
  0.0 197.2 jit_solution(12847813538910238706)
XLA Ops:
  8.0 0.9 convert_element_type.78
  10.9 1.6 scatter_fusion
  12.5 0.9 convert_element_type.79
  13.4 8.5 %all-to-all-start = ((bf16[16,128,128]{2,1,0:T(8,128)(2,1)}), bf16[16,128,128]{2,1,0:T(8,128)(2,1)S(1)}, u32[]{:S(2)}, u32[]{:S(2)}) async-start(bf16[16,128,128]{2,1,0:T(8,128)(2,1)} %convert_element_type.79), calls=%async_computation | async-start | bytes 1048576 | tf_op jit(solution)/shard_map/all_to_all | solution.py:35
  22.0 1.9 all_gather.27
  24.0 1.3 fusion.56
  25.3 11.7 %all-to-all-done = bf16[16,128,128]{2,1,0:T(8,128)(2,1)S(1)} async-done(((bf16[16,128,128]{2,1,0:T(8,128)(2,1)}), bf16[16,128,128]{2,1,0:T(8,128)(2,1)S(1)}, u32[]{:S(2)}, u32[]{:S(2)}) %all-to-all-start) | async-done | bytes 524320 | tf_op jit(solution)/shard_map/all_to_all | solution.py:35
  37.1 1.9 all_gather.24
  43.6 5.9 %reduce-scatter.7.cloned.1.call-done = bf16[128,128]{1,0:T(8,128)(2,1)} async-done(((bf16[256,128]{1,0:T(8,128)(2,1)}), bf16[128,128]{1,0:T(8,128)(2,1)}) %reduce-scatter.7.cloned.1.call-update) | async-done | bytes 32784
  50.4 44.0 %all_gather.25 = bf16[2048,128]{1,0:T(8,128)(2,1)S(1)} all-gather(bf16[128,128]{1,0:T(8,128)(2,1)S(1)} %add_convert_fusion), channel_id=1, replica_groups=mesh['shard'=16,'mp'=2] {'shard'}, dimensions={0}, use_global_device_ids=true | all-gather | bytes 557056 | tf_op jit(solution)/shard_map/all_gather | solution.py:42
  95.4 1.6 scatter_fusion.1
  97.0 2.0 %all_gather.26 = f32[256,256]{1,0:T(8,128)S(1)} all-gather(f32[256,128]{1,0:T(8,128)S(1)} %bitcast.43), channel_id=1, replica_groups=mesh['shard'=16,'mp'=2] {'mp'}, dimensions={1}, use_global_device_ids=true | all-gather | bytes 393216 | tf_op jit(solution)/shard_map/all_gather | solution.py:97
  100.9 2.0 %fusion.2 = f32[256,256]{1,0:T(8,128)S(1)} fusion(bf16[256,1024]{1,0:T(8,128)(2,1)S(1)} %copy-done, f32[256,1024]{1,0:T(8,128)} %fusion.56, bf16[256,1024]{1,0:T(8,128)(2,1)S(1)} %copy-done.21, f32[256,1024]{1,0:T(8,128)S(1)} %fusion.54, f32[256,256]{1,0:T(8,128)S(1)} %all_gather.26, f32[256]{0:T(256)S(1)} %copy-done.20, f32[256]{0:T(256)S(1)} %get-tuple-element.11), kind=kOutput, calls=%fused_computation.11 | convolution fusion | flops 271253504 | bytes 3672064 | tf_op jit(solution)/shard_map/rh,dh->rd/dot_general | solution.py:107
  102.9 1.7 fusion.3
  105.4 3.6 %reduce-scatter.9.cloned.1.call-done = bf16[128,256]{1,0:T(8,128)(2,1)} async-done(((bf16[256,256]{1,0:T(8,128)(2,1)}), bf16[128,256]{1,0:T(8,128)(2,1)}) %reduce-scatter.9.cloned.1.call-update) | async-done | bytes 65552
  109.0 0.9 copy.29
  110.1 2.5 %psum.7 = f32[256]{0:T(256)S(1)} all-reduce(f32[256]{0:T(256)S(1)} %fusion.33), channel_id=1, replica_groups=mesh['shard'=16,'mp'=2] {'mp'}, use_global_device_ids=true, to_apply=%region_8.11 | all-reduce | flops 256 | bytes 2048 | tf_op jit(solution)/shard_map/psum | solution.py:114
  113.9 1.6 scatter_fusion.2
  116.4 6.9 %all-to-all-start.1 = ((bf16[16,128,128]{2,1,0:T(8,128)(2,1)}), bf16[16,128,128]{2,1,0:T(8,128)(2,1)S(1)}, u32[]{:S(2)}, u32[]{:S(2)}) async-start(bf16[16,128,128]{2,1,0:T(8,128)(2,1)} %convert_element_type.92), calls=%async_computation.1 | async-start | bytes 1048576 | tf_op jit(solution)/shard_map/all_to_all | solution.py:35
  123.3 15.4 %all-to-all-done.1 = bf16[16,128,128]{2,1,0:T(8,128)(2,1)S(1)} async-done(((bf16[16,128,128]{2,1,0:T(8,128)(2,1)}), bf16[16,128,128]{2,1,0:T(8,128)(2,1)S(1)}, u32[]{:S(2)}, u32[]{:S(2)}) %all-to-all-start.1) | async-done | bytes 524320 | tf_op jit(solution)/shard_map/all_to_all | solution.py:35
  138.8 2.0 %all_gather.28 = bf16[128,256]{1,0:T(8,128)(2,1)S(1)} all-gather(bf16[128,128]{1,0:T(8,128)(2,1)S(1)} %reduce_sum.76), channel_id=1, replica_groups=mesh['shard'=16,'mp'=2] {'mp'}, dimensions={1}, use_global_device_ids=true | all-gather | bytes 98304 | tf_op jit(solution)/shard_map/all_gather | solution.py:51
  143.4 1.9 all-gather
  145.6 41.2 %all_gather.31 = bf16[2048,128]{1,0:T(8,128)(2,1)S(1)} all-gather(bf16[128,128]{1,0:T(8,128)(2,1)S(1)} %fusion.38), channel_id=1, replica_groups=mesh['shard'=16,'mp'=2] {'shard'}, dimensions={0}, use_global_device_ids=true | all-gather | bytes 557056 | tf_op jit(solution)/shard_map/all_gather | solution.py:42
  187.9 1.6 scatter_fusion.3
  (97 shorter events, 19.2 us)
Async XLA Ops:
  7.2 92.0 %copy-start = (bf16[256,1024]{1,0:T(8,128)(2,1)S(1)}, bf16[256,1024]{1,0:T(8,128)(2,1)}, u32[]{:S(2)}) copy-start(bf16[256,1024]{1,0:T(8,128)(2,1)} %param.31) | copy-start | bytes 1572868
  7.2 0.7 copy-start.19
  8.0 1.0 copy-start.16
  13.4 8.5 %copy-start.13 = (bf16[256,128]{1,0:T(8,128)(2,1)S(1)}, bf16[256,128]{1,0:T(8,128)(2,1)}, u32[]{:S(2)}) copy-start(bf16[256,128]{1,0:T(8,128)(2,1)} %param.22) | copy-start | bytes 196612
  13.4 10.5 %copy-start.10 = (bf16[1024,256]{1,0:T(8,128)(2,1)S(1)}, bf16[1024,256]{1,0:T(8,128)(2,1)}, u32[]{:S(2)}) copy-start(bf16[1024,256]{1,0:T(8,128)(2,1)} %param.33) | copy-start | bytes 1572868
  13.4 23.6 %all-to-all-start = ((bf16[16,128,128]{2,1,0:T(8,128)(2,1)}), bf16[16,128,128]{2,1,0:T(8,128)(2,1)S(1)}, u32[]{:S(2)}, u32[]{:S(2)}) async-start(bf16[16,128,128]{2,1,0:T(8,128)(2,1)} %convert_element_type.79), calls=%async_computation | async-start | bytes 1048576 | tf_op jit(solution)/shard_map/all_to_all | solution.py:35
  21.9 27.6 %reduce-scatter.7.cloned.1.call-start = ((), (), s32[]{:S(2)}) async-start(), calls=%async_computation.4 | async-start | bytes 98304
  25.3 13.8 %copy-start.1 = (bf16[256,1024]{1,0:T(8,128)(2,1)S(1)}, bf16[256,1024]{1,0:T(8,128)(2,1)}, u32[]{:S(2)}) copy-start(bf16[256,1024]{1,0:T(8,128)(2,1)} %param.28) | copy-start | bytes 1572868
  39.1 0.7 copy-start.17
  39.8 1.0 copy-start.3
  40.8 0.8 copy-start.5
  40.8 1.6 copy-start.11
  41.6 0.8 copy-start.7
  43.5 65.5 %reduce-scatter.9.cloned.1.call-start = ((), (), s32[]{:S(2)}) async-start(), calls=%async_computation.5 | async-start | bytes 196608
  99.8 1.0 copy-start.21
  116.4 24.5 %copy-start.12 = (bf16[1024,256]{1,0:T(8,128)(2,1)S(1)}, bf16[1024,256]{1,0:T(8,128)(2,1)}, u32[]{:S(2)}) copy-start(bf16[1024,256]{1,0:T(8,128)(2,1)} %param.30) | copy-start | bytes 1572868
  116.4 22.4 %all-to-all-start.1 = ((bf16[16,128,128]{2,1,0:T(8,128)(2,1)}), bf16[16,128,128]{2,1,0:T(8,128)(2,1)S(1)}, u32[]{:S(2)}, u32[]{:S(2)}) async-start(bf16[16,128,128]{2,1,0:T(8,128)(2,1)} %convert_element_type.92), calls=%async_computation.1 | async-start | bytes 1048576 | tf_op jit(solution)/shard_map/all_to_all | solution.py:35
  138.7 2.4 %copy-start.8 = (f32[128,1024]{1,0:T(8,128)S(1)}, f32[128,1024]{1,0:T(8,128)}, u32[]{:S(2)}) copy-start(f32[128,1024]{1,0:T(8,128)} %copy-done.7) | copy-start | bytes 1572868
  140.8 1.0 copy-start.2
  140.8 1.2 copy-start.6
  142.0 1.0 copy-start.4
  187.9 1.6 copy-start.9
  187.9 1.6 copy-start.14
  187.9 1.6 copy-start.15
  (2 other events, 1.3 us)
Sparse Core Ops, SparseCore 0:
  43.6 5.8 reduce-scatter.6
  105.5 3.4 reduce-scatter.8
